TPU v7x, 32 devices: a whole 2x2x4 slice. The times are simulated.
32 devices in a mesh: seq: 16 (over z, x, core), head: 2 (over y).
Axes of the slice: x: 2, y: 2, z: 4, core: 2. Of those that a mesh axis runs over, the one named last changes fastest.
Arguments:
- old_cache: bfloat16 [1024, 8, 128, 128], P(('seq', 'head')), may hold values from -9 to 9
- page_dest: int32 [1024], P(('seq', 'head')), may hold values from 0 to 1023, as said below
- seq_pages: int32 [32], replicated, may hold values from 1 to 64, 1024 in all
- last_fill: int32 [32], replicated, may hold values from 1 to 128
- queries: bfloat16 [32, 8, 512], P(None, 'head'), may hold values from -16 to 16
Outputs:
- new_cache: bfloat16 [1024, 8, 128, 128], P('seq', 'head')
- attended: bfloat16 [32, 8, 512], P('seq', 'head')
Inputs may be any that keep to these rules, and one draw needn't show every extreme that they name: page_dest is a permutation of the page numbers. The 64 old pages p with the same p // 64 go to exactly 16 distinct new owners page_dest[p] // 64, exactly 4 pages to each; every new owner receives 64 pages.
All inputs are finite; a program needn't handle non-finite values.
Results may differ from a plain program's by a relative error of at most 0.004.
Values may be sent and summed in bfloat16 or wider, within the bound.
No kernel may reach another device: no remote copies, remote signals or barrier semaphores. Data moves between devices by JAX's collectives and lax.ppermute only.
A program may use at most 64 MiB of HBM per device.

v0:
```python
import jax
import jax.numpy as jnp
from jax import lax
from jax.sharding import PartitionSpec as P

NEG_FILL = -1e30


def page_layout(index_new, seq_pages, last_fill, seq_total, page_len, page_count, seq_peers):
    position = index_new % page_count * seq_peers + index_new // page_count
    seq_ends = jnp.cumsum(seq_pages)
    page_owner = jnp.sum((position[:, None] >= seq_ends[None, :]).astype(jnp.int32), axis=1)
    member = page_owner[:, None] == jnp.arange(seq_total, dtype=jnp.int32)[None, :]
    owner_end = jnp.sum(jnp.where(member, seq_ends[None, :], 0), axis=1)
    owner_fill = jnp.sum(jnp.where(member, last_fill[None, :], 0), axis=1)
    page_fill = jnp.where(position == owner_end - 1, owner_fill, page_len)
    token_live = jnp.arange(page_len, dtype=jnp.int32)[None, :] < page_fill[:, None]
    return (member, token_live)


def local_scores(page_block, member, token_live, queries):
    page_count, head_count, page_len, double = page_block.shape
    head_width = double // 2
    group_size = queries.shape[2] // head_width
    page_query = jnp.dot(
        member.astype(jnp.bfloat16),
        queries.reshape(queries.shape[0], -1),
        preferred_element_type=jnp.float32,
    ).astype(jnp.bfloat16)
    page_query = page_query.reshape(page_count, head_count, group_size, head_width)
    scores = jnp.einsum(
        "pkgd,pktd->pkgt",
        page_query,
        page_block[..., :head_width],
        preferred_element_type=jnp.float32,
    ) * head_width ** (-0.5)
    scores = jnp.where(token_live[:, None, None, :], scores, NEG_FILL)
    page_max = jnp.max(scores, axis=3)
    seq_local = jnp.max(jnp.where(member.T[:, :, None, None], page_max[None], NEG_FILL), axis=1)
    return (scores, seq_local.reshape(queries.shape[0], -1))


def partial_sums(page_block, member, token_live, scores, seq_max):
    page_count = page_block.shape[0]
    head_width = page_block.shape[3] // 2
    member_float = member.astype(jnp.float32)
    owner_max = jnp.dot(member_float, seq_max, precision=lax.Precision.HIGHEST).reshape(
        scores.shape[:3]
    )
    weights = jnp.where(
        token_live[:, None, None, :], jnp.exp(scores - owner_max[..., None]), 0.0
    ).astype(jnp.bfloat16)
    page_total = jnp.sum(weights.astype(jnp.float32), axis=3)
    page_sum = jnp.einsum(
        "pkgt,pktd->pkgd", weights, page_block[..., head_width:], preferred_element_type=jnp.float32
    )
    totals = jnp.dot(
        member_float.T, page_total.reshape(page_count, -1), precision=lax.Precision.HIGHEST
    )
    weighted = jnp.dot(
        member_float.T, page_sum.reshape(page_count, -1), precision=lax.Precision.HIGHEST
    )
    return (weighted, totals)


def route_pages(page_block, index_new, seq_peers):
    page_count = page_block.shape[0]
    slot_cap = page_count // min(seq_peers, 16)
    target = index_new // page_count
    slot_new = index_new % page_count
    order_ids = jnp.arange(page_count, dtype=jnp.int32)
    earlier = (target[None, :] == target[:, None]) & (order_ids[None, :] < order_ids[:, None])
    position = target * slot_cap + jnp.sum(earlier.astype(jnp.int32), axis=1)
    matches = position[None, :] == jnp.arange(seq_peers * slot_cap, dtype=jnp.int32)[:, None]
    source = jnp.sum(jnp.where(matches, order_ids[None, :], 0), axis=1)
    filled = jnp.any(matches, axis=1)
    outgoing = jnp.where(
        filled[:, None, None, None],
        jnp.take(page_block, source, axis=0),
        jnp.zeros((), jnp.bfloat16),
    )
    labels = jnp.where(filled, jnp.take(slot_new, source), -1).astype(jnp.int32)
    return (
        outgoing.reshape((seq_peers, slot_cap) + page_block.shape[1:]),
        labels.reshape(seq_peers, slot_cap),
    )


def move_pages(outgoing, labels, page_count):
    incoming, tag_list = (
        lax.all_to_all(outgoing, "seq", split_axis=0, concat_axis=0, tiled=True),
        lax.all_to_all(labels, "seq", split_axis=0, concat_axis=0, tiled=True),
    )
    flat_pages = incoming.reshape((-1,) + incoming.shape[2:])
    flat_labels = tag_list.reshape(-1)
    slot_ids = jnp.arange(flat_labels.shape[0], dtype=jnp.int32)
    matches = flat_labels[None, :] == jnp.arange(page_count, dtype=jnp.int32)[:, None]
    anchor = jnp.sum(jnp.where(matches, slot_ids[None, :], 0), axis=1)
    return jnp.take(flat_pages, anchor, axis=0)


def per_device(old_cache, page_dest, seq_pages, last_fill, queries):
    spread = jnp.broadcast_to(page_dest[:, None], (page_dest.shape[0], old_cache.shape[1]))
    regrouped, spread_back = (
        lax.all_to_all(old_cache, "head", split_axis=1, concat_axis=0, tiled=True),
        lax.all_to_all(spread, "head", split_axis=1, concat_axis=0, tiled=True),
    )
    index_old = spread_back[:, 0]
    page_count = regrouped.shape[0]
    page_len = regrouped.shape[2]
    head_count = regrouped.shape[1]
    head_width = regrouped.shape[3] // 2
    seq_peers = lax.axis_size("seq")
    seq_total = queries.shape[0]
    outgoing, labels = route_pages(regrouped, index_old, seq_peers)
    member, token_live = page_layout(
        index_old, seq_pages, last_fill, seq_total, page_len, page_count, seq_peers
    )
    scores, seq_local = local_scores(regrouped, member, token_live, queries)
    new_cache = move_pages(outgoing, labels, page_count)
    seq_max = lax.pmax(seq_local, "seq")
    weighted, totals = partial_sums(regrouped, member, token_live, scores, seq_max)
    local_seqs = seq_total // seq_peers
    weighted, totals = lax.psum((weighted, totals), "seq")
    first_row = lax.axis_index("seq") * local_seqs
    weighted = lax.dynamic_slice_in_dim(weighted, first_row, local_seqs, 0)
    totals = lax.dynamic_slice_in_dim(totals, first_row, local_seqs, 0)
    result = weighted.reshape(local_seqs, -1, head_width) / totals[:, :, None]
    attended = result.reshape(local_seqs, head_count, -1).astype(jnp.bfloat16)
    return (new_cache, attended)


def solution(mesh):
    in_specs = (
        P(("seq", "head"), None, None, None),
        P(("seq", "head")),
        P(),
        P(),
        P(None, "head", None),
    )
    out_specs = (P("seq", "head", None, None), P("seq", "head", None))
    return jax.shard_map(
        per_device, mesh=mesh, in_specs=in_specs, out_specs=out_specs, check_vma=False
    )
```

profile of v0, /device:TPU:0, one launch (start us, length us, event | category | flops | bytes accessed | tf_op | source)
XLA Modules:
  0.0 517.2 jit_solution(4860052772208484157)
XLA Ops:
  7.8 0.6 reshape.291
  8.5 4.3 all-to-all-start
  12.7 10.5 %copy.33 = bf16[32,8,128,128]{3,2,0,1:T(8,128)(2,1)} copy(bf16[32,8,128,128]{3,2,1,0:T(8,128)(2,1)} %param.7) | data formatting | bytes 16777216 | tf_op args[0]
  23.3 6.9 %all-to-all-start.1 = ((bf16[32,8,128,128]{3,2,0,1:T(8,128)(2,1)}), bf16[32,8,128,128]{3,2,0,1:T(8,128)(2,1)}, u32[]{:S(2)}, u32[]{:S(2)}) async-start(bf16[32,8,128,128]{3,2,0,1:T(8,128)(2,1)} %copy.33), calls=%async_computation.1 | async-start | bytes 16777216 | tf_op jit(solution)/shard_map/all_to_all | solution.py:105
  30.7 0.7 reduce.5
  32.0 0.8 gather_fusion
  33.7 89.3 %all-to-all-done.1 = bf16[32,8,128,128]{3,2,0,1:T(8,128)(2,1)} async-done(((bf16[32,8,128,128]{3,2,0,1:T(8,128)(2,1)}), bf16[32,8,128,128]{3,2,0,1:T(8,128)(2,1)}, u32[]{:S(2)}, u32[]{:S(2)}) %all-to-all-start.1) | async-done | bytes 8388640 | tf_op jit(solution)/shard_map/all_to_all | solution.py:105
  123.0 6.1 %all-to-all-start.3 = ((s32[16,1,4]{2,1,0:T(1,128)}), s32[16,1,4]{2,1,0:T(1,128)S(1)}, u32[]{:S(2)}, u32[]{:S(2)}) async-start(s32[16,1,4]{2,1,0:T(1,128)} %bitcast.5), calls=%async_computation.3 | async-start | bytes 16384 | tf_op jit(solution)/shard_map/all_to_all | solution.py:92
  129.2 12.0 %copy.34 = bf16[32,2,4,128,128]{3,4,2,0,1:T(8,128)(2,1)} copy(bf16[32,2,4,128,128]{4,3,0,2,1:T(8,128)(2,1)} %bitcast.6) | data formatting | bytes 16777216 | tf_op jit(solution)/shard_map/all_to_all | solution.py:105
  141.1 8.9 %gather_fusion.1 = bf16[64,4,128,128]{2,3,1,0:T(8,128)(2,1)} fusion(bf16[64,4,128,128]{2,3,1,0:T(8,128)(2,1)} %bitcast.54, s32[1024]{0:T(1024)S(1)} %pad_clamp_fusion.1), kind=kCustom, calls=%fused_computation.clone | custom fusion | bytes 16777472 | tf_op jit(solution)/shard_map/jit(_take)/gather | solution.py:79
  150.0 7.6 %select_select_fusion = bf16[64,4,128,128]{2,3,1,0:T(8,128)(2,1)} fusion(bf16[64,4,128,128]{2,3,1,0:T(8,128)(2,1)} %gather_fusion.1, pred[64]{0:T(512)(128)(4,1)S(1)} %compare_and_fusion.1, pred[64]{0:T(512)(128)(4,1)S(1)} %fusion.10), kind=kLoop, calls=%fused_computation.3 | loop fusion | flops 8388608 | bytes 16777344 | tf_op jit(solution)/shard_map/jit(_where)/select_n | solution.py:77
  157.7 6.2 %all-to-all-start.2 = ((bf16[16,4,4,128,128]{3,4,2,1,0:T(8,128)(2,1)}), bf16[16,4,4,128,128]{3,4,2,1,0:T(8,128)(2,1)}, u32[]{:S(2)}, u32[]{:S(2)}) async-start(bf16[16,4,4,128,128]{3,4,2,1,0:T(8,128)(2,1)} %bitcast.58), calls=%async_computation.2 | async-start | bytes 16777216 | tf_op jit(solution)/shard_map/all_to_all | solution.py:91
  165.8 0.7 reduce.4
  166.8 3.6 fusion.24
  170.8 214.5 %pmax.7 = f32[32,32]{0,1:T(8,128)S(1)} all-reduce(f32[32,32]{0,1:T(8,128)S(1)} %bitcast.61), channel_id=1, replica_groups=mesh['seq'=16,'head'=2] {'seq'}, use_global_device_ids=true, to_apply=%region_10.12 | all-reduce | flops 1024 | bytes 8192 | tf_op jit(solution)/shard_map/pmax | solution.py:121
  385.5 4.6 fusion
  390.4 1.0 fusion.14
  391.5 0.8 convert_reduce_fusion
  392.5 57.9 %psum.15 = f32[32,32]{1,0:T(8,128)S(1)} all-reduce(f32[32,32]{1,0:T(8,128)S(1)} %fusion.12), channel_id=1, replica_groups=mesh['seq'=16,'head'=2] {'seq'}, use_global_device_ids=true, to_apply=%region_13.15 | all-reduce | flops 1024 | bytes 8192 | tf_op jit(solution)/shard_map/psum | solution.py:124
  450.5 29.6 %all-reduce.2.cloned.1.call-done = f32[32,2048]{1,0:T(8,128)} async-done(((f32[32,2048]{1,0:T(8,128)}), f32[32,2048]{1,0:T(8,128)}) %all-reduce.2.cloned.1.call-update) | async-done | bytes 262160 | tf_op jit(solution)/shard_map/psum | solution.py:124
  480.0 0.8 constant_dynamic-slice_fusion.1
  481.5 12.2 %copy.35 = bf16[16,4,4,128,128]{4,3,2,1,0:T(8,128)(2,1)} copy(bf16[16,4,4,128,128]{3,4,2,1,0:T(8,128)(2,1)} %all-to-all-done.2) | data formatting | bytes 16777216 | tf_op jit(solution)/shard_map/all_to_all | solution.py:91
  493.8 8.9 %gather_fusion.2 = bf16[64,4,128,128]{3,2,1,0:T(8,128)(2,1)} fusion(bf16[64,4,128,128]{3,2,1,0:T(8,128)(2,1)} %bitcast.57, s32[1024]{0:T(1024)S(1)} %pad_clamp_fusion), kind=kCustom, calls=%fused_computation.1.clone | custom fusion | bytes 16777472 | tf_op jit(solution)/shard_map/jit(_take)/gather | solution.py:99
  502.7 7.6 %broadcast_select_fusion = bf16[64,4,128,128]{3,2,1,0:T(8,128)(2,1)} fusion(bf16[64,4,128,128]{3,2,1,0:T(8,128)(2,1)} %gather_fusion.2, pred[64]{0:T(512)(128)(4,1)S(1)} %compare_and_fusion), kind=kLoop, calls=%fused_computation.4 | loop fusion | flops 4194304 | bytes 16777280 | tf_op jit(solution)/shard_map/jit(_take)/select_n | solution.py:99
  (67 shorter events, 6.9 us)
Async XLA Ops:
  7.2 0.7 copy-start
  8.5 14.8 %all-to-all-start = ((s32[2,1,128]{2,1,0:T(1,128)}), s32[2,1,128]{2,1,0:T(1,128)S(1)}, u32[]{:S(2)}, u32[]{:S(2)}) async-start(s32[2,1,128]{2,1,0:T(1,128)} %reshape.291), calls=%async_computation | async-start | bytes 2048 | tf_op jit(solution)/shard_map/all_to_all | solution.py:106
  23.3 99.8 %all-to-all-start.1 = ((bf16[32,8,128,128]{3,2,0,1:T(8,128)(2,1)}), bf16[32,8,128,128]{3,2,0,1:T(8,128)(2,1)}, u32[]{:S(2)}, u32[]{:S(2)}) async-start(bf16[32,8,128,128]{3,2,0,1:T(8,128)(2,1)} %copy.33), calls=%async_computation.1 | async-start | bytes 16777216 | tf_op jit(solution)/shard_map/all_to_all | solution.py:105
  123.0 34.6 %all-to-all-start.3 = ((s32[16,1,4]{2,1,0:T(1,128)}), s32[16,1,4]{2,1,0:T(1,128)S(1)}, u32[]{:S(2)}, u32[]{:S(2)}) async-start(s32[16,1,4]{2,1,0:T(1,128)} %bitcast.5), calls=%async_computation.3 | async-start | bytes 16384 | tf_op jit(solution)/shard_map/all_to_all | solution.py:92
  157.6 6.3 %copy-start.3 = (s32[32]{0:T(128)S(1)}, s32[32]{0:T(128)}, u32[]{:S(2)}) copy-start(s32[32]{0:T(128)} %param.9) | copy-start | bytes 388
  157.6 6.5 %copy-start.2 = (bf16[32,4,512]{2,1,0:T(4,128)(2,1)S(1)}, bf16[32,4,512]{2,1,0:T(4,128)(2,1)}, u32[]{:S(2)}) copy-start(bf16[32,4,512]{2,1,0:T(4,128)(2,1)} %param.11) | copy-start | bytes 393220
  157.7 7.5 %copy-start.4 = (s32[32]{0:T(128)S(1)}, s32[32]{0:T(128)}, u32[]{:S(2)}) copy-start(s32[32]{0:T(128)} %param.10) | copy-start | bytes 388
  157.7 323.9 %all-to-all-start.2 = ((bf16[16,4,4,128,128]{3,4,2,1,0:T(8,128)(2,1)}), bf16[16,4,4,128,128]{3,4,2,1,0:T(8,128)(2,1)}, u32[]{:S(2)}, u32[]{:S(2)}) async-start(bf16[16,4,4,128,128]{3,4,2,1,0:T(8,128)(2,1)} %bitcast.58), calls=%async_computation.2 | async-start | bytes 16777216 | tf_op jit(solution)/shard_map/all_to_all | solution.py:91
  163.9 316.2 %all-reduce.2.cloned.1.call-start = ((), (), s32[]{:S(2)}) async-start(), calls=%async_computation.4 | async-start | bytes 524288 | tf_op jit(solution)/shard_map/psum | solution.py:124
  493.8 16.6 %copy-start.1 = (s32[32]{0:T(128)S(1)}, s32[32]{0:T(128)}, u32[]{:S(2)}) copy-start(s32[32]{0:T(128)} %param.8) | copy-start | bytes 388
Sparse Core Ops, SparseCore 0:
  391.6 88.3 all-reduce.1
where the time goes:
time: 518 us; the launch traced here: 517 us
  blocking collectives  272 us (53%)
  waiting for transfers between devices  119 us (23%)
  local copies, waits for them, and re-layouts  58.6 us (11%)
  starting transfers between devices  23.5 us (5%)
  other arithmetic  19.9 us (4%)
  between operations  14.3 us (3%)
  matrix products  9.67 us (2%)
    pmax x1, blocking collectives, per_device(): seq_max = lax.pmax(seq_local, 'seq')  214 us
    all_to_all x1, waiting for transfers between devices, per_device(): lax.all_to_all(old_cache, 'head', split_axis=1, concat_axis=0, tiled=True)  89.3 us
    psum x1, blocking collectives, per_device(): weighted, totals = lax.psum((weighted, totals), 'seq')  57.9 us
    psum x1, waiting for transfers between devices, per_device(): weighted, totals = lax.psum((weighted, totals), 'seq')  29.6 us
    all_to_all x1, local copies, waits for them, and re-layouts, move_pages(): lax.all_to_all(outgoing, 'seq', split_axis=0, concat_axis=0, tiled=True)  12.2 us
    all_to_all x1, local copies, waits for them, and re-layouts, per_device(): lax.all_to_all(old_cache, 'head', split_axis=1, concat_axis=0, tiled=True)  12 us
    unnamed x15, local copies, waits for them, and re-layouts  11.9 us
  transfers between devices with their start and end apart: 5, of which 2 were waited for; matrix products, arithmetic and copies ran while one was open for 11% of the time, Pallas kernels for 0%

commit v1 on v0

v1 whole, which is shorter than its diff:
```python
import functools
import jax
import jax.numpy as jnp
from jax import lax
from jax.experimental import pallas as pl
from jax.experimental.pallas import tpu as pltpu
from jax.sharding import PartitionSpec as P

NEG_FILL = -1e30
LABEL_ROWS = 8

ANY = pl.BlockSpec(memory_space=pl.ANY)
SMEM = pl.BlockSpec(memory_space=pltpu.SMEM)
VMEM = pl.BlockSpec(memory_space=pltpu.VMEM)


def chunk_rows(rows):
    eighths = (1, 3, 4)
    unit = rows // 8
    edges, start = [], 0
    for share in eighths:
        edges.append((start, share * unit))
        start += share * unit
    return edges


def pack_kernel(sizes, *refs):
    pages_own, page_count, peers, cap, rows, start, length, groups, extra, label = sizes
    dest, head_id, old = refs[:3]
    received = refs[3:3 + groups - 1]
    refs = refs[3 + groups - 1:]
    tail = None
    if extra and not label:
        tail, refs = refs[0], refs[1:]
    out, stage, counts, places, slots, label_tile, in_sem, out_sem, tail_sem = refs
    offset = pl.multiple_of(head_id[0] * rows + start, 8)
    copies = [pltpu.make_async_copy(
        old.at[:, pl.ds(offset, length), :], stage.at[pl.ds(0, pages_own)], in_sem.at[0])]
    for j, block in enumerate(received):
        copies.append(pltpu.make_async_copy(
            block, stage.at[pl.ds((j + 1) * pages_own, pages_own)], in_sem.at[j + 1]))
    for copy in copies:
        copy.start()
    if tail is not None:
        tail_copy = pltpu.make_async_copy(
            tail, out.at[:, pl.ds(cap * length, extra), :], tail_sem)
        tail_copy.start()

    @pl.loop(0, peers)
    def _(t):
        counts[t] = 0

    if label:
        @pl.loop(0, peers * cap)
        def _(i):
            slots[i] = -1

    @pl.loop(0, page_count)
    def _(p):
        d = dest[p]
        t = d // page_count
        n = counts[t]
        counts[t] = n + 1
        places[p] = t * cap + n
        if label:
            slots[t * cap + n] = d - t * page_count

    def page_copy(p):
        place = places[p]
        t = place // cap
        row = pl.multiple_of((place - t * cap) * length, 8)
        return pltpu.make_async_copy(
            stage.at[p], out.at[t, pl.ds(row, length), :], out_sem.at[p])

    if label:
        lane = lax.broadcasted_iota(jnp.int32, (extra, 128), 1)

        @pl.loop(0, peers)
        def _(t):
            tile = jnp.full((extra, 128), -1, jnp.int32)
            for n in range(cap):
                tile = jnp.where(lane == n, slots[t * cap + n], tile)
            label_tile[t] = tile.astype(jnp.float32).astype(jnp.bfloat16)

        tail_copy = pltpu.make_async_copy(
            label_tile, out.at[:, pl.ds(cap * length, extra), :], tail_sem)
        tail_copy.start()
    for j in range(groups):
        copies[j].wait()

        @pl.loop(j * pages_own, (j + 1) * pages_own)
        def _(p):
            page_copy(p).start()

    @pl.loop(0, page_count)
    def _(p):
        page_copy(p).wait()

    if extra:
        tail_copy.wait()


def pack(dest, head_id, old, received, tail, geometry, start, length, label):
    pages_own, page_count, peers, cap, rows, groups = geometry
    extra = LABEL_ROWS if label else (tail.shape[1] if tail is not None else 0)
    sizes = (pages_own, page_count, peers, cap, rows, start, length, groups, extra, label)
    operands = [dest, head_id, old, *received] + ([tail] if tail is not None else [])
    specs = [SMEM, SMEM] + [ANY] * groups + ([VMEM] if tail is not None else [])
    moved = 4 * page_count * length * 128
    return pl.pallas_call(
        functools.partial(pack_kernel, sizes),
        out_shape=jax.ShapeDtypeStruct((peers, cap * length + extra, 128), jnp.bfloat16),
        in_specs=specs,
        out_specs=ANY,
        scratch_shapes=[
            pltpu.VMEM((page_count, length, 128), jnp.bfloat16),
            pltpu.SMEM((peers,), jnp.int32),
            pltpu.SMEM((page_count,), jnp.int32),
            pltpu.SMEM((peers * cap,), jnp.int32),
            pltpu.VMEM((peers, LABEL_ROWS, 128), jnp.bfloat16),
            pltpu.SemaphoreType.DMA((groups,)),
            pltpu.SemaphoreType.DMA((page_count,)),
            pltpu.SemaphoreType.DMA,
        ],
        cost_estimate=pl.CostEstimate(flops=moved * 4, bytes_accessed=moved, transcendentals=0),
        name="pack",
    )(*operands)


def merge_partials(tail, attended, peers, local, width, rows):
    lane = lax.broadcasted_iota(jnp.int32, (rows, 128), 1)
    row = lax.broadcasted_iota(jnp.int32, (rows, 128), 0)
    diagonal = lane == row
    parts = local * rows
    for s in range(local):
        logs = []
        top = jnp.full((rows, 1), NEG_FILL, jnp.float32)
        for t in range(peers):
            scale_rows = tail[t, parts:parts + 8, :].astype(jnp.float32)
            line = jnp.sum(scale_rows[3 * s:3 * s + 3], axis=0, keepdims=True)
            line = jnp.where(diagonal, jnp.broadcast_to(line, (rows, 128)), 0.0)
            value = jnp.sum(line, axis=1, keepdims=True)
            logs.append(value)
            top = jnp.maximum(top, value)
        total = jnp.zeros((rows, 1), jnp.float32)
        summed = jnp.zeros((rows, 128), jnp.float32)
        for t in range(peers):
            scale = jnp.exp(logs[t] - top)
            total = total + scale
            summed = summed + scale * tail[t, s * rows:(s + 1) * rows, :].astype(jnp.float32)
        values = summed[:, width:] + summed[:, :width]
        attended[s] = (values / total).astype(jnp.bfloat16)


def place_kernel(sizes, *refs):
    _, peers, cap, start, length, extra, first, local, width, rows = sizes
    labels, incoming = refs[:2]
    refs = refs[2:] if first else refs[3:]
    cache = refs[0]
    refs = refs[1:]
    if extra:
        attended, refs = refs[0], refs[1:]
    stage, in_sem, out_sem = refs[:3]
    if extra:
        tail, tail_sem = refs[3:]
        tail_copy = pltpu.make_async_copy(
            incoming.at[:, pl.ds(cap * length, extra), :], tail, tail_sem)
        tail_copy.start()

    def block_copy(t):
        return pltpu.make_async_copy(
            incoming.at[t, pl.ds(0, cap * length), :], stage.at[t], in_sem.at[t])

    def page_copy(t, n):
        i = t * cap + n
        return pltpu.make_async_copy(
            stage.at[t, pl.ds(n * length, length), :],
            cache.at[labels[i], pl.ds(start, length), :], out_sem.at[i])

    @pl.loop(0, peers)
    def _(t):
        block_copy(t).start()

    @pl.loop(0, peers)
    def _(t):
        block_copy(t).wait()
        for n in range(cap):
            @pl.when(labels[t * cap + n] >= 0)
            def _():
                page_copy(t, n).start()

    if extra:
        tail_copy.wait()
        merge_partials(tail, attended, peers, local, width, rows)

    @pl.loop(0, peers)
    def _(t):
        for n in range(cap):
            @pl.when(labels[t * cap + n] >= 0)
            def _():
                page_copy(t, n).wait()


def place(labels, incoming, cache, geometry, start, length, merged):
    _, page_count, peers, cap, rows, _ = geometry
    local, kj, width = merged if merged else (0, 0, 0)
    extra = incoming.shape[1] - cap * length if merged else 0
    first = cache is None
    sizes = (page_count, peers, cap, start, length, extra, first, local, width, kj)
    operands = [labels, incoming] + ([] if first else [cache])
    outs = [jax.ShapeDtypeStruct((page_count, rows, 128), jnp.bfloat16)]
    out_specs = [ANY]
    scratch = [
        pltpu.VMEM((peers, cap * length, 128), jnp.bfloat16),
        pltpu.SemaphoreType.DMA((peers,)),
        pltpu.SemaphoreType.DMA((peers * cap,)),
    ]
    if extra:
        outs.append(jax.ShapeDtypeStruct((local, kj, width), jnp.bfloat16))
        out_specs.append(VMEM)
        scratch += [pltpu.VMEM((peers, extra, 128), jnp.bfloat16), pltpu.SemaphoreType.DMA]
    moved = 4 * page_count * length * 128
    return pl.pallas_call(
        functools.partial(place_kernel, sizes),
        out_shape=outs,
        in_specs=[SMEM, ANY] + ([] if first else [ANY]),
        out_specs=out_specs,
        scratch_shapes=scratch,
        input_output_aliases={} if first else {2: 0},
        cost_estimate=pl.CostEstimate(flops=moved * 4, bytes_accessed=moved, transcendentals=0),
        name="place",
    )(*operands)


def attend_kernel(sizes, *refs):
    pages_own, page_count, peers, rows, groups, chunks, kj, width, page_len, local = sizes
    owner, fill, head_id, query, old = refs[:5]
    blocks = refs[5:5 + len(chunks) * (groups - 1)]
    (out, stage, tile_max, tile_total, tile_sum,
     seq_max, seq_total, seq_sum, sems) = refs[5 + len(blocks):]
    heads = rows // page_len
    group = kj // heads
    offset = pl.multiple_of(head_id[0] * rows, 8)
    copies = [pltpu.make_async_copy(
        old.at[:, pl.ds(offset, rows), :], stage.at[pl.ds(0, pages_own)], sems.at[0])]
    for j in range(groups - 1):
        for c, (start, length) in enumerate(chunks):
            i = j * len(chunks) + c
            copies.append(pltpu.make_async_copy(
                blocks[i],
                stage.at[pl.ds((j + 1) * pages_own, pages_own), pl.ds(start, length), :],
                sems.at[i + 1]))
    for copy in copies:
        copy.start()
    seq_max[...] = jnp.full_like(seq_max, NEG_FILL)
    seq_total[...] = jnp.zeros_like(seq_total)
    seq_sum[...] = jnp.zeros_like(seq_sum)
    for copy in copies:
        copy.wait()
    token = lax.broadcasted_iota(jnp.int32, (group, page_len), 1)
    scale = width ** -0.5

    @pl.loop(0, page_count, unroll=2)
    def _(p):
        s = owner[p]
        live = token < fill[p]
        for k in range(heads):
            page = stage[p, k * page_len:(k + 1) * page_len, :]
            q = query[s, k * group:(k + 1) * group, :]
            scores = lax.dot_general(
                q, page, (((1,), (1,)), ((), ())), preferred_element_type=jnp.float32) * scale
            scores = jnp.where(live, scores, NEG_FILL)
            top = jnp.max(scores, axis=1, keepdims=True)
            weights = jnp.where(live, jnp.exp(scores - top), 0.0).astype(jnp.bfloat16)
            total = jnp.sum(weights.astype(jnp.float32), axis=1, keepdims=True)
            here = pl.ds(k * group, group)
            tile_sum[p, here, :] = jnp.dot(weights, page, preferred_element_type=jnp.float32)
            tile_max[p, here, :] = jnp.broadcast_to(top, (group, 128))
            tile_total[p, here, :] = jnp.broadcast_to(total, (group, 128))

    @pl.loop(0, page_count)
    def _(p):
        s = owner[p]
        seq_max[s] = jnp.maximum(seq_max[s], tile_max[p])

    @pl.loop(0, page_count)
    def _(p):
        s = owner[p]
        factor = jnp.exp(tile_max[p] - seq_max[s])
        seq_total[s] = seq_total[s] + factor * tile_total[p]
        seq_sum[s] = seq_sum[s] + factor * tile_sum[p]

    lane = lax.broadcasted_iota(jnp.int32, (kj, 128), 1)
    diagonal = lane == lax.broadcasted_iota(jnp.int32, (kj, 128), 0)
    parts = local * kj

    @pl.loop(0, peers)
    def _(t):
        lines = []
        for i in range(local):
            s = t * local + i
            total = seq_total[s]
            some = total > 0.0
            safe = jnp.where(some, total, 1.0)
            value = jnp.where(some, seq_sum[s] / safe, 0.0)
            high = value.astype(jnp.bfloat16).astype(jnp.float32)
            low = pltpu.roll(value - high, 128 - width, 1)
            out[t, i * kj:(i + 1) * kj, :] = jnp.where(lane < width, low, high).astype(jnp.bfloat16)
            log = jnp.where(some, seq_max[s] + jnp.log(safe), NEG_FILL)
            for _ in range(3):
                part = log.astype(jnp.bfloat16).astype(jnp.float32)
                log = log - part
                lines.append(jnp.sum(jnp.where(diagonal, part, 0.0), axis=0, keepdims=True))
        while len(lines) % 8:
            lines.append(jnp.zeros((1, 128), jnp.float32))
        out[t, parts:parts + len(lines), :] = jnp.concatenate(lines, 0).astype(jnp.bfloat16)


def attend(owner, fill, head_id, query, old, received, geometry, chunks, width, page_len):
    pages_own, page_count, peers, _, rows, groups = geometry
    seqs, kj, _ = query.shape
    local = seqs // peers
    extra = local * kj + (3 * local + 7) // 8 * 8
    blocks = [received[c][j] for j in range(groups - 1) for c in range(len(chunks))]
    sizes = (pages_own, page_count, peers, rows, groups, chunks, kj, width, page_len, local)
    return pl.pallas_call(
        functools.partial(attend_kernel, sizes),
        out_shape=jax.ShapeDtypeStruct((peers, extra, 128), jnp.bfloat16),
        in_specs=[SMEM, SMEM, SMEM, VMEM, ANY] + [ANY] * len(blocks),
        out_specs=VMEM,
        scratch_shapes=[
            pltpu.VMEM((page_count, rows, 128), jnp.bfloat16),
            pltpu.VMEM((page_count, kj, 128), jnp.float32),
            pltpu.VMEM((page_count, kj, 128), jnp.float32),
            pltpu.VMEM((page_count, kj, 128), jnp.float32),
            pltpu.VMEM((seqs, kj, 128), jnp.float32),
            pltpu.VMEM((seqs, kj, 128), jnp.float32),
            pltpu.VMEM((seqs, kj, 128), jnp.float32),
            pltpu.SemaphoreType.DMA((len(blocks) + 1,)),
        ],
        cost_estimate=pl.CostEstimate(
            flops=page_count * kj * page_len * 512 * 16, bytes_accessed=2 * page_count * rows * 128,
            transcendentals=page_count * kj * page_len),
        name="attend",
    )(owner, fill, head_id, query, old, *blocks)


def page_layout(dest, seq_pages, last_fill, page_len, page_count, peers):
    position = dest % page_count * peers + dest // page_count
    seqs = seq_pages.shape[0]
    ids = jnp.arange(seqs, dtype=jnp.int32)
    ends = jnp.sum(jnp.where(ids[:, None] <= ids[None, :], seq_pages[:, None], 0), axis=0)
    owner = jnp.sum((position[:, None] >= ends[None, :]).astype(jnp.int32), axis=1)
    member = owner[:, None] == ids[None, :]
    last = jnp.any(member & (position[:, None] == ends[None, :] - 1), axis=1)
    owner_fill = jnp.sum(jnp.where(member, last_fill[None, :], 0), axis=1)
    return owner, jnp.where(last, owner_fill, page_len)


def per_device(old_cache, page_dest, seq_pages, last_fill, queries):
    pages_own, all_heads, page_len, double = old_cache.shape
    groups = lax.axis_size("head")
    peers = lax.axis_size("seq")
    head = lax.axis_index("head").astype(jnp.int32)
    width = double // 2
    heads = all_heads // groups
    rows = heads * page_len
    page_count = pages_own * groups
    cap = page_count // min(peers, 16)
    seqs = queries.shape[0]
    kj = heads * (queries.shape[2] // width)
    geometry = (pages_own, page_count, peers, cap, rows, groups)
    chunks = tuple(chunk_rows(rows))
    old = old_cache.reshape(pages_own, all_heads * page_len, double)
    head_id = head[None]

    def shift(x, j):
        return lax.ppermute(x, "head", [(i, (i + j) % groups) for i in range(groups)])

    received, source = [], old
    dests = [page_dest]
    for c, (start, length) in enumerate(chunks):
        pieces = []
        for j in range(1, groups):
            target = (head + j) % groups
            pieces.append(lax.dynamic_slice(
                source, (0, target * rows + start, 0), (pages_own, length, double)))
        source, pieces = lax.optimization_barrier((source, pieces))
        received.append([shift(piece, j) for j, piece in enumerate(pieces, 1)])
        if c == 0:
            dests += [shift(page_dest, j) for j in range(1, groups)]
    dest = jnp.concatenate(dests)
    query = jnp.pad(queries.reshape(seqs, kj, width), ((0, 0), (0, 0), (0, double - width)))
    owner, fill = page_layout(dest, seq_pages, last_fill, page_len, page_count, peers)
    cache = labels = None
    for c, (start, length) in enumerate(chunks):
        final = c == len(chunks) - 1
        tail = None
        if final:
            tail = attend(owner, fill, head_id, query, old, received, geometry, chunks,
                          width, page_len)
        outgoing = pack(dest, head_id, old, received[c], tail, geometry, start, length, c == 0)
        incoming = lax.all_to_all(outgoing, "seq", split_axis=0, concat_axis=0, tiled=True)
        if c == 0:
            labels = incoming[:, cap * length, :cap].astype(jnp.int32).reshape(-1)
        merged = (seqs // peers, kj, width) if final else None
        outs = place(labels, incoming, cache, geometry, start, length, merged)
        cache = outs[0]
    attended = outs[1].reshape(seqs // peers, heads, -1)
    return cache.reshape(page_count, heads, page_len, double), attended


def solution(mesh):
    in_specs = (
        P(("seq", "head"), None, None, None),
        P(("seq", "head")),
        P(),
        P(),
        P(None, "head", None),
    )
    out_specs = (P("seq", "head", None, None), P("seq", "head", None))
    return jax.shard_map(
        per_device, mesh=mesh, in_specs=in_specs, out_specs=out_specs, check_vma=False
    )
```

time: 518 us -> 321 us (0.62)
  the two profiles are of different devices: /device:TPU:0 before, /device:TPU:11 now
where the time goes in v1:
time: 321 us; the launch traced here: 320 us
  waiting for transfers between devices  180 us (56%)
  Pallas kernels  98.4 us (31%)
  starting transfers between devices  25.3 us (8%)
  local copies, waits for them, and re-layouts  13.4 us (4%)
    all_to_all x3, waiting for transfers between devices, per_device(): lax.all_to_all(outgoing, 'seq', split_axis=0, concat_axis=0, tiled=True)  89.9 us
    ppermute x4, waiting for transfers between devices, shift(): lax.ppermute(x, 'head', [(i, (i + j) % groups) for i in range(groups)])  89.6 us
    pallas_call x1, Pallas kernels, attend(): pl.pallas_call(functools.partial(attend_kernel, sizes), out_shape=jax.Sha...  71.3 us
    all_to_all x3, starting transfers between devices, per_device(): lax.all_to_all(outgoing, 'seq', split_axis=0, concat_axis=0, tiled=True)  21.2 us
    pallas_call x3, Pallas kernels, pack(): pl.pallas_call(functools.partial(pack_kernel, sizes), out_shape=jax.Shape...  13.8 us
    pallas_call x3, Pallas kernels, place(): pl.pallas_call(functools.partial(place_kernel, sizes), out_shape=outs, in...  13.3 us
  transfers between devices with their start and end apart: 7, of which 4 were waited for; matrix products, arithmetic and copies ran while one was open for 3% of the time, Pallas kernels for 28%

profile of v1, /device:TPU:11, one launch (start us, length us, event | category | flops | bytes accessed | tf_op | source)
XLA Modules:
  0.0 320.3 jit_solution(16715974522748241548)
XLA Ops:
  0.6 1.1 constant_dynamic-slice_fusion.2
  1.7 1.3 collective-permute-start.1
  3.3 11.4 %collective-permute-done = s32[32]{0:T(128)S(1)} collective-permute-done((s32[32]{0:T(128)}, s32[32]{0:T(128)S(1)}, u32[]{:S(2)}, u32[]{:S(2)}) %collective-permute-start) | collective-permute-done | bytes 160 | tf_op jit(solution)/shard_map/ppermute | solution.py:378
  14.6 1.2 fusion.4
  16.7 4.3 %pack.3 = bf16[16,264,128]{2,1,0:T(8,128)(2,1)} custom-call(s32[64]{0:T(128)} %get-tuple-element.17.refs_0_, s32[1]{0:T(128)} %bitcast.refs_1_.refs_2_, bf16[32,1024,128]{2,1,0:T(8,128)(2,1)} %bitcast.4, bf16[32,64,128]{2,1,0:T(8,128)(2,1)} %copy-done.3), custom_call_target="tpu_custom_call" | custom-call | flops 8388608 | bytes 2097152 | tf_op jit(solution)/shard_map/pack/pallas_call | solution.py:110
  21.0 7.5 %all-to-all-start = ((bf16[16,264,128]{2,1,0:T(8,128)(2,1)}), bf16[16,264,128]{2,1,0:T(8,128)(2,1)S(1)}, u32[]{:S(2)}, u32[]{:S(2)}) async-start(bf16[16,264,128]{2,1,0:T(8,128)(2,1)} %pack.3), calls=%async_computation | async-start | bytes 2162688 | tf_op jit(solution)/shard_map/all_to_all | solution.py:403
  28.4 1.5 constant_dynamic-slice_fusion.1
  30.0 1.3 collective-permute-start.3
  31.3 34.3 %collective-permute-done.3.refs_6_.refs_3_ = bf16[32,192,128]{2,1,0:T(8,128)(2,1)S(1)} collective-permute-done((bf16[32,192,128]{2,1,0:T(8,128)(2,1)S(1)}, bf16[32,192,128]{2,1,0:T(8,128)(2,1)S(1)}, u32[]{:S(2)}, u32[]{:S(2)}) %collective-permute-start.3) | collective-permute-done | bytes 1572896 | tf_op jit(solution)/shard_map/ppermute | solution.py:378
  65.6 1.2 copy-done.1
  66.8 4.3 %pack.5 = bf16[16,768,128]{2,1,0:T(8,128)(2,1)} custom-call(s32[64]{0:T(128)} %get-tuple-element.17.refs_0_, s32[1]{0:T(128)} %bitcast.refs_1_.refs_2_, bf16[32,1024,128]{2,1,0:T(8,128)(2,1)} %bitcast.6, bf16[32,192,128]{2,1,0:T(8,128)(2,1)} %copy-done.1), custom_call_target="tpu_custom_call" | custom-call | flops 25165824 | bytes 6291456 | tf_op jit(solution)/shard_map/pack/pallas_call | solution.py:110
  72.1 6.9 %all-to-all-start.2 = ((bf16[16,768,128]{2,1,0:T(8,128)(2,1)}), bf16[16,768,128]{2,1,0:T(8,128)(2,1)S(1)}, u32[]{:S(2)}, u32[]{:S(2)}) async-start(bf16[16,768,128]{2,1,0:T(8,128)(2,1)} %pack.5), calls=%async_computation.2 | async-start | bytes 6291456 | tf_op jit(solution)/shard_map/all_to_all | solution.py:403
  79.0 3.2 %constant_dynamic-slice_fusion = bf16[32,256,128]{2,1,0:T(8,128)(2,1)} fusion(bf16[32,1024,128]{2,1,0:T(8,128)(2,1)} %bitcast.7, s32[]{:T(128)S(6)} %select_n.54), kind=kLoop, calls=%fused_computation.14 | loop fusion | bytes 4194308 | tf_op jit(solution)/shard_map/dynamic_slice | solution.py:386
  82.2 1.2 collective-permute-start.2
  85.4 43.9 %collective-permute-done.2.refs_7_.refs_3_ = bf16[32,256,128]{2,1,0:T(8,128)(2,1)} collective-permute-done((bf16[32,256,128]{2,1,0:T(8,128)(2,1)}, bf16[32,256,128]{2,1,0:T(8,128)(2,1)}, u32[]{:S(2)}, u32[]{:S(2)}) %collective-permute-start.2) | collective-permute-done | bytes 2097184 | tf_op jit(solution)/shard_map/ppermute | solution.py:378
  129.3 71.3 %attend.1.refs_4_ = bf16[16,72,128]{2,1,0:T(8,128)(2,1)} custom-call(s32[64]{0:T(128)} %copy-done.5, s32[64]{0:T(128)} %broadcast_select_fusion.refs_1_, s32[1]{0:T(128)} %bitcast.refs_1_.refs_2_, bf16[32,32,128]{2,1,0:T(8,128)(2,1)} %pad.4.refs_3_, bf16[32,1024,128]{2,1,0:T(8,128)(2,1)} %bitcast.8, bf16[32,64,128]{2,1,0:T(8,128)(2,1)} %copy-done.3, ...), custom_call_target="tpu_custom_call" | custom-call | flops 2147483648 | bytes 8388608 | tf_op jit(solution)/shard_map/attend/pallas_call | solution.py:326
  200.6 5.2 %pack.4 = bf16[16,1096,128]{2,1,0:T(8,128)(2,1)} custom-call(s32[64]{0:T(128)} %get-tuple-element.17.refs_0_, s32[1]{0:T(128)} %bitcast.refs_1_.refs_2_, bf16[32,1024,128]{2,1,0:T(8,128)(2,1)} %bitcast.9, bf16[32,256,128]{2,1,0:T(8,128)(2,1)} %collective-permute-done.2.refs_7_.refs_3_, bf16[16,72,128]{2,1,0:T(8,128)(2,1)} %attend.1.refs_4_), custom_call_target="tpu_custom_call" | custom-call | flops 33554432 | bytes 8388608 | tf_op jit(solution)/shard_map/pack/pallas_call | solution.py:110
  205.9 1.6 copy-done
  207.5 6.9 %all-to-all-start.1 = ((bf16[16,1096,128]{2,1,0:T(8,128)(2,1)}), bf16[16,1096,128]{2,1,0:T(8,128)(2,1)}, u32[]{:S(2)}, u32[]{:S(2)}) async-start(bf16[16,1096,128]{2,1,0:T(8,128)(2,1)} %pack.4), calls=%async_computation.1 | async-start | bytes 8978432 | tf_op jit(solution)/shard_map/all_to_all | solution.py:403
  215.7 3.3 %place.3.refs_2_ = bf16[64,512,128]{2,1,0:T(8,128)(2,1)} custom-call(s32[64]{0:T(128)} %reshape.146.refs_0_, bf16[16,264,128]{2,1,0:T(8,128)(2,1)} %copy-done.2), custom_call_target="tpu_custom_call" | custom-call | flops 8388608 | bytes 2097152 | tf_op jit(solution)/shard_map/place/pallas_call | solution.py:223
  219.0 4.3 %place.4.refs_2_ = bf16[64,512,128]{2,1,0:T(8,128)(2,1)} custom-call(s32[64]{0:T(128)} %reshape.146.refs_0_, bf16[16,768,128]{2,1,0:T(8,128)(2,1)} %copy-done, bf16[64,512,128]{2,1,0:T(8,128)(2,1)} %place.3.refs_2_), custom_call_target="tpu_custom_call", output_to_operand_aliasing={{}: (2, {})} | custom-call | flops 25165824 | bytes 6291456 | tf_op jit(solution)/shard_map/place/pallas_call | solution.py:223
  223.3 89.9 %all-to-all-done.1.refs_1_ = bf16[16,1096,128]{2,1,0:T(8,128)(2,1)} async-done(((bf16[16,1096,128]{2,1,0:T(8,128)(2,1)}), bf16[16,1096,128]{2,1,0:T(8,128)(2,1)}, u32[]{:S(2)}, u32[]{:S(2)}) %all-to-all-start.1) | async-done | bytes 4489248 | tf_op jit(solution)/shard_map/all_to_all | solution.py:403
  313.1 5.8 %place.5 = (bf16[64,512,128]{2,1,0:T(8,128)(2,1)}, bf16[2,32,64]{2,1,0:T(8,128)(2,1)}) custom-call(s32[64]{0:T(128)} %reshape.146.refs_0_, bf16[16,1096,128]{2,1,0:T(8,128)(2,1)} %all-to-all-done.1.refs_1_, bf16[64,512,128]{2,1,0:T(8,128)(2,1)} %place.4.refs_2_), custom_call_target="tpu_custom_call", output_to_operand_aliasing={{0}: (2, {})} | custom-call | flops 33554432 | bytes 8388608 | tf_op jit(solution)/shard_map/place/pallas_call | solution.py:223
  318.9 1.4 reshape.145
  (28 shorter events, 5.3 us)
Async XLA Ops:
  1.7 14.1 %collective-permute-start.1 = (bf16[32,64,128]{2,1,0:T(8,128)(2,1)S(1)}, bf16[32,64,128]{2,1,0:T(8,128)(2,1)S(1)}, u32[]{:S(2)}, u32[]{:S(2)}) collective-permute-start(bf16[32,64,128]{2,1,0:T(8,128)(2,1)S(1)} %constant_dynamic-slice_fusion.2), channel_id=1, source_target_pairs={{0,1},{1,0},{2,3},{3,2},{4,5},{5,4},{6,7},{7,6},{8,9},{9,8},{10,11... | collective-permute-start | bytes 1572872 | tf_op jit(solution)/shard_map/ppermute | solution.py:378
  3.0 11.6 %collective-permute-start = (s32[32]{0:T(128)}, s32[32]{0:T(128)S(1)}, u32[]{:S(2)}, u32[]{:S(2)}) collective-permute-start(s32[32]{0:T(128)} %param.6), channel_id=1, source_target_pairs={{0,1},{1,0},{2,3},{3,2},{4,5},{5,4},{6,7},{7,6},{8,9},{9,8},{10,11... | collective-permute-start | bytes 392 | tf_op jit(solution)/shard_map/ppermute | solution.py:378
  15.9 0.8 copy-start.3
  21.0 50.1 %all-to-all-start = ((bf16[16,264,128]{2,1,0:T(8,128)(2,1)}), bf16[16,264,128]{2,1,0:T(8,128)(2,1)S(1)}, u32[]{:S(2)}, u32[]{:S(2)}) async-start(bf16[16,264,128]{2,1,0:T(8,128)(2,1)} %pack.3), calls=%async_computation | async-start | bytes 2162688 | tf_op jit(solution)/shard_map/all_to_all | solution.py:403
  30.0 35.6 %collective-permute-start.3 = (bf16[32,192,128]{2,1,0:T(8,128)(2,1)S(1)}, bf16[32,192,128]{2,1,0:T(8,128)(2,1)S(1)}, u32[]{:S(2)}, u32[]{:S(2)}) collective-permute-start(bf16[32,192,128]{2,1,0:T(8,128)(2,1)S(1)} %constant_dynamic-slice_fusion.1), channel_id=1, source_target_pairs={{0,1},{1,0},{2,3},{3,2},{4,5},{5,4},{6,7},{7,6},{8,9},{9,8},{10,11... | collective-permute-start | bytes 4718600 | tf_op jit(solution)/shard_map/ppermute | solution.py:378
  65.6 1.2 copy-start.1
  71.1 1.0 copy-start.2
  72.1 133.8 %all-to-all-start.2 = ((bf16[16,768,128]{2,1,0:T(8,128)(2,1)}), bf16[16,768,128]{2,1,0:T(8,128)(2,1)S(1)}, u32[]{:S(2)}, u32[]{:S(2)}) async-start(bf16[16,768,128]{2,1,0:T(8,128)(2,1)} %pack.5), calls=%async_computation.2 | async-start | bytes 6291456 | tf_op jit(solution)/shard_map/all_to_all | solution.py:403
  78.9 4.5 %copy-start.4 = (bf16[32,4,512]{2,1,0:T(4,128)(2,1)S(1)}, bf16[32,4,512]{2,1,0:T(4,128)(2,1)}, u32[]{:S(2)}) copy-start(bf16[32,4,512]{2,1,0:T(4,128)(2,1)} %param.9) | copy-start | bytes 393220
  79.0 5.4 %copy-start.6 = (s32[32]{0:T(128)S(1)}, s32[32]{0:T(128)}, u32[]{:S(2)}) copy-start(s32[32]{0:T(128)} %param.7) | copy-start | bytes 388
  79.0 5.6 %copy-start.7 = (s32[32]{0:T(128)S(1)}, s32[32]{0:T(128)}, u32[]{:S(2)}) copy-start(s32[32]{0:T(128)} %param.8) | copy-start | bytes 388
  82.2 47.1 %collective-permute-start.2 = (bf16[32,256,128]{2,1,0:T(8,128)(2,1)}, bf16[32,256,128]{2,1,0:T(8,128)(2,1)}, u32[]{:S(2)}, u32[]{:S(2)}) collective-permute-start(bf16[32,256,128]{2,1,0:T(8,128)(2,1)} %constant_dynamic-slice_fusion), channel_id=1, source_target_pairs={{0,1},{1,0},{2,3},{3,2},{4,5},{5,4},{6,7},{7,6},{8,9},{9,8},{10,11... | collective-permute-start | bytes 6291464 | tf_op jit(solution)/shard_map/ppermute | solution.py:378
  84.6 44.7 %copy-start.5 = (s32[64]{0:T(128)}, s32[64]{0:T(128)S(1)}, u32[]{:S(2)}) copy-start(s32[64]{0:T(128)S(1)} %convert_reduce_fusion.refs_0_) | copy-start | bytes 772
  205.9 1.6 copy-start
  207.5 105.6 %all-to-all-start.1 = ((bf16[16,1096,128]{2,1,0:T(8,128)(2,1)}), bf16[16,1096,128]{2,1,0:T(8,128)(2,1)}, u32[]{:S(2)}, u32[]{:S(2)}) async-start(bf16[16,1096,128]{2,1,0:T(8,128)(2,1)} %pack.4), calls=%async_computation.1 | async-start | bytes 8978432 | tf_op jit(solution)/shard_map/all_to_all | solution.py:403
